TPU v7x, 32 devices: a whole 2x2x4 slice. The times are simulated.
32 devices in a mesh: groups: 2 (over y), seq: 16 (over z, x, core).
Axes of the slice: x: 2, y: 2, z: 4, core: 2. Of those that a mesh axis runs over, the one named last changes fastest.
Arguments:
- queries: bfloat16 [8192, 4096], P(('groups', 'seq')), parts along dimension 0
- new_keys: bfloat16 [8192, 1024], P(('groups', 'seq')), parts along dimension 0
- new_values: bfloat16 [8192, 1024], P(('groups', 'seq')), parts along dimension 0, may hold values from -6 to 6
- pool_keys: bfloat16 [672, 16, 1024], P(('groups', 'seq')), parts along dimension 0, may hold values from -10 to 10
- pool_values: bfloat16 [672, 16, 1024], P(('groups', 'seq')), parts along dimension 0, may hold values from -6 to 6
- prefix_len: int32 [32], P(('groups', 'seq')), parts along dimension 0, may hold values from 1 to 80
- new_len: int32 [32], P(('groups', 'seq')), parts along dimension 0, may hold values from 128 to 256
- page_holder: int32 [32, 5], P(('groups', 'seq')), parts along dimension 0, may hold values from 0 to 15, as said below
- page_slot: int32 [32, 5], P(('groups', 'seq')), parts along dimension 0, may hold values from 0 to 20, as said below
- new_holder: int32 [32, 16], P(('groups', 'seq')), parts along dimension 0, may hold values from 0 to 15, as said below
- new_slot: int32 [32, 16], P(('groups', 'seq')), parts along dimension 0, may hold values from 0 to 20
Outputs:
- attention_out: bfloat16 [8192, 4096], P(('groups', 'seq')), parts along dimension 0
- pool_keys_out: bfloat16 [672, 16, 1024], P(('groups', 'seq')), parts along dimension 0
- pool_values_out: bfloat16 [672, 16, 1024], P(('groups', 'seq')), parts along dimension 0
There are 2 independent parts, one for each index of `groups`. A program takes and returns all parts, laid end to end along the dimension named above; each array names one. Nothing has to cross between parts.
Inputs may be any that keep to these rules, and one draw needn't show every extreme that they name: `page_holder`: the 5 pages named for one conversation lie on distinct devices. No pool slot is named twice by page_slot and new_slot together, and no slot named by new_slot is named by page_slot. `new_holder`: the 16 pages of one conversation's new turn go to distinct devices.
All inputs are finite; a program needn't handle non-finite values.
Results may differ from a plain program's by a relative error of at most 0.0027.
Values may be sent and summed in bfloat16 or wider, within the bound.
A program may use at most 128 MiB of HBM per device.

v0:
```python
import functools
import math

import jax
import jax.numpy as jnp
from jax import lax
from jax.experimental import pallas as pl
from jax.experimental.pallas import tpu as pltpu
from jax.sharding import PartitionSpec as P

HEADS = 32
KV_HEADS = 8
HEAD = 128
ROWS = 128
SLOT_LANE = 64
EARLY = 5
MESH = pl.DeviceIdType.MESH


def kernel(
    n,
    new_pages,
    prefix_pages,
    prefix_len,
    new_len,
    page_holder,
    page_slot,
    new_holder,
    new_slot,
    q_hbm,
    k_hbm,
    v_hbm,
    pk_hbm,
    pv_hbm,
    out,
    recv_new,
    pool,
    source,
    q,
    kv,
    prefix,
    send_new,
    send_pre,
    recv_pre,
    meta,
    recv_meta,
    tables,
    in_sem,
    table_sem,
    meta_send_sem,
    meta_recv_sem,
    new_send_sem,
    new_recv_sem,
    pre_send_sem,
    pre_recv_sem,
):
    me = lax.axis_index("seq")
    mine = lax.axis_index("groups")
    span = q.shape[0]
    page_rows = pool.shape[2]
    slots = pool.shape[1]
    group = HEADS // KV_HEADS

    loads = [
        pltpu.make_async_copy(k_hbm, kv.at[0], in_sem.at[0]),
        pltpu.make_async_copy(v_hbm, kv.at[1], in_sem.at[1]),
        pltpu.make_async_copy(pk_hbm, pool.at[0], in_sem.at[2]),
        pltpu.make_async_copy(pv_hbm, pool.at[1], in_sem.at[3]),
        pltpu.make_async_copy(q_hbm, q, in_sem.at[4]),
    ]
    for load in loads:
        load.start()

    def peer(step):
        return lax.rem(me + step, n)

    barrier = pltpu.get_barrier_semaphore()

    def greet(step, carry):
        pl.semaphore_signal(barrier, inc=1, device_id=(mine, peer(step)), device_id_type=MESH)
        return carry

    lax.fori_loop(1, n, greet, 0)

    lanes = lax.broadcasted_iota(jnp.int32, meta.shape, 1)
    row = jnp.full(meta.shape, -1, jnp.int32)
    for i in range(new_pages):
        row = jnp.where(lanes == i, new_holder[0, i], row)
        row = jnp.where(lanes == SLOT_LANE + i, new_slot[0, i], row)
    for j in range(prefix_pages):
        row = jnp.where(lanes == new_pages + j, page_holder[0, j], row)
        row = jnp.where(lanes == SLOT_LANE + new_pages + j, page_slot[0, j], row)
    meta[...] = row
    recv_meta[me] = row

    prefix[...] = jnp.zeros_like(prefix)
    live = new_len[0]
    loads[0].wait()
    loads[1].wait()
    page_pos = lax.broadcasted_iota(jnp.int32, (page_rows, kv.shape[3]), 0)

    def fill_new(target, carry):
        page = jnp.int32(0)
        for i in range(new_pages):
            page = jnp.where(new_holder[0, i] == target, i, page)
        keep = page_pos < live - page * page_rows
        for side in range(2):
            rows = kv[side, page]
            send_new[target, side] = jnp.where(keep, rows, jnp.zeros_like(rows))
        return carry

    lax.fori_loop(0, n, fill_new, 0)
    recv_new[me] = send_new[me]

    def meta_copy(step):
        return pltpu.make_async_remote_copy(
            src_ref=meta,
            dst_ref=recv_meta.at[me],
            send_sem=meta_send_sem.at[step],
            recv_sem=meta_recv_sem.at[me],
            device_id=(mine, peer(step)),
            device_id_type=MESH,
        )

    def page_copy(step, sent, received, send_sem, recv_sem):
        return pltpu.make_async_remote_copy(
            src_ref=sent.at[peer(step)],
            dst_ref=received.at[me],
            send_sem=send_sem.at[step],
            recv_sem=recv_sem.at[me],
            device_id=(mine, peer(step)),
            device_id_type=MESH,
        )

    def new_copy(step):
        return page_copy(step, send_new, recv_new, new_send_sem, new_recv_sem)

    def pre_copy(step):
        return page_copy(step, send_pre, recv_pre, pre_send_sem, pre_recv_sem)

    def arrival(step, buffer, sem):
        at = peer(step)
        return pltpu.make_async_copy(buffer.at[at], buffer.at[at], sem.at[at])

    pl.semaphore_wait(barrier, n - 1)

    def each(first, last, act):
        def body(step, carry):
            act(step)
            return carry

        lax.fori_loop(first, last, body, 0)

    each(1, n, lambda step: meta_copy(step).start())
    early = min(EARLY, n - 1) + 1
    each(1, early, lambda step: new_copy(step).start())
    loads[2].wait()
    loads[3].wait()
    each(1, n, lambda step: arrival(step, recv_meta, meta_recv_sem).wait())
    table_copy = pltpu.make_async_copy(recv_meta, tables, table_sem)
    table_copy.start()
    table_copy.wait()

    def fill_pre(target):
        slot = jnp.int32(0)
        for j in range(prefix_pages):
            slot = jnp.where(
                tables[target, 0, new_pages + j] == me,
                tables[target, 0, SLOT_LANE + new_pages + j],
                slot,
            )
        for side in range(2):
            send_pre[target, side] = pool[side, slot]

    def ask(step):
        fill_pre(peer(step))

    ask(1)

    def pipelined(step):
        ask(step)
        pre_copy(step - 1).start()

    each(2, n, pipelined)
    fill_pre(me)
    pre_copy(n - 1).start()
    recv_pre[me] = send_pre[me]
    each(early, n, lambda step: new_copy(step).start())

    def clear(slot):
        source[slot] = -1

    each(0, slots, clear)

    def incoming(device, carry):
        landing = jnp.int32(-1)
        for i in range(new_pages):
            landing = jnp.where(
                tables[device, 0, i] == me, tables[device, 0, SLOT_LANE + i], landing
            )

        for slot in range(slots):
            source[slot] = jnp.where(landing == slot, device, source[slot])
        return carry

    lax.fori_loop(0, n, incoming, 0)
    loads[4].wait()

    each(1, n, lambda step: arrival(step, recv_pre, pre_recv_sem).wait())
    for j in range(prefix_pages):
        for side in range(2):
            prefix[side, j * page_rows : (j + 1) * page_rows, :] = recv_pre[page_holder[0, j], side]

    factor = math.log2(math.e) / math.sqrt(HEAD)
    nt = (((1,), (1,)), ((), ()))
    row_pos = lax.rem(lax.broadcasted_iota(jnp.int32, (group * ROWS, ROWS), 0), ROWS)
    col_pos = lax.broadcasted_iota(jnp.int32, (group * ROWS, ROWS), 1)
    prefix_pos = lax.broadcasted_iota(jnp.int32, (group * ROWS, prefix.shape[1]), 1)
    prefix_tokens = prefix_len[0]

    def head_cols(g, h):
        return pl.ds(pl.multiple_of((g * group + h) * HEAD, HEAD), HEAD)

    def attend(g):
        kv_cols = pl.ds(pl.multiple_of(g * HEAD, HEAD), HEAD)
        for block in range(span // ROWS):
            rows = slice(block * ROWS, (block + 1) * ROWS)
            keys = (block + 1) * ROWS
            query = jnp.concatenate(
                [q[rows, head_cols(g, h)] for h in range(group)], axis=0
            )
            old = lax.dot_general(
                query, prefix[0, :, kv_cols], nt, preferred_element_type=jnp.float32
            )
            fresh = lax.dot_general(
                query,
                kv[0, : keys // page_rows, :, kv_cols].reshape(keys, HEAD),
                nt,
                preferred_element_type=jnp.float32,
            )
            old = jnp.where(prefix_pos < prefix_tokens, old, -jnp.inf)
            last = jnp.where(col_pos <= row_pos, fresh[:, block * ROWS :], -jnp.inf)
            parts = [fresh[:, i * ROWS : (i + 1) * ROWS] for i in range(block)] + [last]
            top = old
            for part in parts:
                top = jnp.maximum(top, part)
            top = jnp.max(top, axis=1, keepdims=True)
            old = jnp.exp2((old - top) * factor)
            parts = [jnp.exp2((part - top) * factor) for part in parts]
            total = old
            for part in parts:
                total = total + part
            total = jnp.sum(total, axis=1, keepdims=True)
            weighted = jnp.dot(
                old.astype(jnp.bfloat16),
                prefix[1, :, kv_cols],
                preferred_element_type=jnp.float32,
            )
            weighted = weighted + jnp.dot(
                jnp.concatenate(parts, axis=1).astype(jnp.bfloat16),
                kv[1, : keys // page_rows, :, kv_cols].reshape(keys, HEAD),
                preferred_element_type=jnp.float32,
            )
            result = weighted * (1.0 / total)
            result = jnp.where(row_pos + block * ROWS < live, result, 0.0).astype(jnp.bfloat16)
            for h in range(group):
                out[rows, head_cols(g, h)] = result[h * ROWS : (h + 1) * ROWS]

    each(0, KV_HEADS, attend)

    each(1, n, lambda step: arrival(step, recv_new, new_recv_sem).wait())
    each(1, n, lambda step: meta_copy(step).wait_send())
    each(1, n, lambda step: new_copy(step).wait_send())
    each(1, n, lambda step: pre_copy(step).wait_send())


def finish(source, out, recv_new, pool, o_hbm, pko_hbm, pvo_hbm, pool_out, sem):
    slots = pool.shape[1]
    whole = pltpu.make_async_copy(out, o_hbm, sem.at[0])
    whole.start()

    def place(slot, carry):
        device = source[slot]
        found = device >= 0
        for side in range(2):
            pool_out[side, slot] = jnp.where(
                found, recv_new[jnp.maximum(device, 0), side], pool[side, slot]
            )
        return carry

    lax.fori_loop(0, slots, place, 0)
    stores = [
        pltpu.make_async_copy(pool_out.at[0], pko_hbm, sem.at[1]),
        pltpu.make_async_copy(pool_out.at[1], pvo_hbm, sem.at[2]),
    ]
    for store in stores:
        store.start()
    for store in stores:
        store.wait()
    whole.wait()


def shards(
    queries,
    new_keys,
    new_values,
    pool_keys,
    pool_values,
    prefix_len,
    new_len,
    page_holder,
    page_slot,
    new_holder,
    new_slot,
):
    n = lax.axis_size("seq")
    slots, page_rows, width = pool_keys.shape
    span = queries.shape[0]
    new_pages = new_holder.shape[1]
    prefix_pages = page_holder.shape[1]
    padded = -(-prefix_pages * page_rows // ROWS) * ROWS
    kind = queries.dtype
    smem = pl.BlockSpec(memory_space=pltpu.SMEM)
    anywhere = pl.BlockSpec(memory_space=pl.ANY)
    exchange = pltpu.VMEM((n, 2, page_rows, width), kind)
    peers = pltpu.SemaphoreType.DMA((n,))
    held = pl.BlockSpec(memory_space=pltpu.VMEM)
    page_bytes = 2 * page_rows * width * kind.itemsize
    kept = queries.size * kind.itemsize + (n + slots) * page_bytes
    grant = 67043328 - kept - 256 * 1024
    results = (
        jax.ShapeDtypeStruct(queries.shape, kind),
        jax.ShapeDtypeStruct(pool_keys.shape, kind),
        jax.ShapeDtypeStruct(pool_values.shape, kind),
    )
    out, recv_new, pool, source = pl.pallas_call(
        functools.partial(kernel, n, new_pages, prefix_pages),
        out_shape=(
            pltpu.VMEM(queries.shape, kind),
            pltpu.VMEM((n, 2, page_rows, width), kind),
            pltpu.VMEM((2, slots, page_rows, width), kind),
            jax.ShapeDtypeStruct((slots,), jnp.int32),
        ),
        in_specs=[smem] * 6 + [anywhere] * 5,
        out_specs=(held, held, held, smem),
        scratch_shapes=[
            pltpu.VMEM(queries.shape, kind),
            pltpu.VMEM((2, span // page_rows, page_rows, width), kind),
            pltpu.VMEM((2, padded, width), kind),
            exchange,
            exchange,
            exchange,
            pltpu.VMEM((1, 128), jnp.int32),
            pltpu.VMEM((n, 1, 128), jnp.int32),
            pltpu.SMEM((n, 1, 128), jnp.int32),
            pltpu.SemaphoreType.DMA((5,)),
            pltpu.SemaphoreType.DMA,
            peers,
            peers,
            peers,
            peers,
            peers,
            peers,
        ],
        compiler_params=pltpu.CompilerParams(
            collective_id=0, has_side_effects=True, vmem_limit_bytes=grant
        ),
    )(
        prefix_len,
        new_len,
        page_holder,
        page_slot,
        new_holder,
        new_slot,
        queries,
        new_keys.reshape(span // page_rows, page_rows, width),
        new_values.reshape(span // page_rows, page_rows, width),
        pool_keys,
        pool_values,
    )
    return pl.pallas_call(
        finish,
        out_shape=results,
        in_specs=[smem, held, held, held],
        out_specs=(anywhere,) * 3,
        scratch_shapes=[
            pltpu.VMEM((2, slots, page_rows, width), kind),
            pltpu.SemaphoreType.DMA((3,)),
        ],
        compiler_params=pltpu.CompilerParams(
            vmem_limit_bytes=slots * page_bytes + 4 * 1024 * 1024
        ),
    )(source, out, recv_new, pool)


def solution(mesh):
    rows = P(("groups", "seq"), None)
    pages = P(("groups", "seq"), None, None)
    each = P(("groups", "seq"))
    return jax.shard_map(
        shards,
        mesh=mesh,
        in_specs=(rows, rows, rows, pages, pages, each, each, rows, rows, rows, rows),
        out_specs=(rows, pages, pages),
        check_vma=False,
    )
```

profile of v0, /device:TPU:11, one launch (start us, length us, event | category | flops | bytes accessed | tf_op | source)
XLA Modules:
  0.0 58.8 jit_solution(494588472637419132)
XLA Ops:
  1.9 53.9 %shard_map.130 = (bf16[256,4096]{1,0:T(8,128)(2,1)S(1)}, bf16[16,2,16,1024]{3,2,1,0:T(8,128)(2,1)S(1)}, bf16[2,21,16,1024]{3,2,1,0:T(8,128)(2,1)S(1)}, s32[21]{0:T(128)}) custom-call(s32[1]{0:T(128)S(6)} %copy.14.prefix_len, s32[1]{0:T(128)S(6)} %copy.15.new_len, s32[1,5]{1,0:T(1,128)} %page_holder.1, s32[1,5]{1,0:T(1,128)} %page_slot.1, ...), custom_call_target="tpu_custom_call" | custom-call | tf_op jit(solution)/shard_map/pallas_call | solution.py:336
  55.8 0.0 copy-start
  55.8 0.6 %copy-done = s32[21]{0:T(128)S(1)} copy-done((s32[21]{0:T(128)S(1)}, s32[21]{0:T(128)}, u32[]{:S(2)}) %copy-start) | copy-done | bytes 108
  56.4 2.3 %shard_map.131 = (bf16[256,4096]{1,0:T(8,128)(2,1)}, bf16[21,16,1024]{2,1,0:T(8,128)(2,1)}, bf16[21,16,1024]{2,1,0:T(8,128)(2,1)}) custom-call(s32[21]{0:T(128)S(1)} %copy-done, bf16[256,4096]{1,0:T(8,128)(2,1)S(1)} %get-tuple-element.8.out, bf16[16,2,16,1024]{3,2,1,0:T(8,128)(2,1)S(1)} %get-tuple-element.9.recv_new, ...), custom_call_target="tpu_custom_call" | custom-call | tf_op jit(solution)/shard_map/pallas_call | solution.py:381
Async XLA Ops:
  55.8 0.6 %copy-start = (s32[21]{0:T(128)S(1)}, s32[21]{0:T(128)}, u32[]{:S(2)}) copy-start(s32[21]{0:T(128)} %get-tuple-element.7.source) | copy-start | bytes 256
where the time goes:
time: 58.9 us; the launch traced here: 58.8 us
  Pallas kernels  56.2 us (95%)
  between operations  1.94 us (3%)
  local copies, waits for them, and re-layouts  0.62 us (1%)
    pallas_call x1, Pallas kernels, shards(): pl.pallas_call(functools.partial(kernel, n, new_pages, prefix_pages), out...  53.9 us
    pallas_call x1, Pallas kernels, shards(): pl.pallas_call(finish, out_shape=results, in_specs=[smem, held, held, hel...  2.33 us

commit v1 on v0

--- a/solution.py
+++ b/solution.py
@@ -14,7 +14,12 @@
 ROWS = 128
 SLOT_LANE = 64
 EARLY = 5
+FIRST = 1
 MESH = pl.DeviceIdType.MESH
+
+
+def crosses_once(n, new_pages):
+    return n == new_pages and n % 4 == 0
 
 
 def kernel(
@@ -40,8 +45,6 @@
     kv,
     prefix,
     send_new,
-    send_pre,
-    recv_pre,
     meta,
     recv_meta,
     tables,
@@ -51,11 +54,11 @@
     meta_recv_sem,
     new_send_sem,
     new_recv_sem,
-    pre_send_sem,
-    pre_recv_sem,
+    *exchange,
 ):
     me = lax.axis_index("seq")
     mine = lax.axis_index("groups")
+    halves = crosses_once(n, new_pages)
     span = q.shape[0]
     page_rows = pool.shape[2]
     slots = pool.shape[1]
@@ -112,35 +115,36 @@
     lax.fori_loop(0, n, fill_new, 0)
     recv_new[me] = send_new[me]
 
-    def meta_copy(step):
+    def remote(sent, received, send_sem, recv_sem, target):
         return pltpu.make_async_remote_copy(
-            src_ref=meta,
-            dst_ref=recv_meta.at[me],
-            send_sem=meta_send_sem.at[step],
-            recv_sem=meta_recv_sem.at[me],
-            device_id=(mine, peer(step)),
+            src_ref=sent,
+            dst_ref=received,
+            send_sem=send_sem,
+            recv_sem=recv_sem,
+            device_id=(mine, target),
             device_id_type=MESH,
         )
 
-    def page_copy(step, sent, received, send_sem, recv_sem):
-        return pltpu.make_async_remote_copy(
-            src_ref=sent.at[peer(step)],
-            dst_ref=received.at[me],
-            send_sem=send_sem.at[step],
-            recv_sem=recv_sem.at[me],
-            device_id=(mine, peer(step)),
-            device_id_type=MESH,
+    def landed(buffer, sem):
+        return pltpu.make_async_copy(buffer, buffer, sem)
+
+    def meta_copy(step):
+        return remote(
+            meta, recv_meta.at[me], meta_send_sem.at[step], meta_recv_sem.at[me], peer(step)
         )
 
-    def new_copy(step):
-        return page_copy(step, send_new, recv_new, new_send_sem, new_recv_sem)
-
-    def pre_copy(step):
-        return page_copy(step, send_pre, recv_pre, pre_send_sem, pre_recv_sem)
+    def new_to(target):
+        return remote(
+            send_new.at[target],
+            recv_new.at[me],
+            new_send_sem.at[target],
+            new_recv_sem.at[me],
+            target,
+        )
 
     def arrival(step, buffer, sem):
         at = peer(step)
-        return pltpu.make_async_copy(buffer.at[at], buffer.at[at], sem.at[at])
+        return landed(buffer.at[at], sem.at[at])
 
     pl.semaphore_wait(barrier, n - 1)
 
@@ -152,64 +156,282 @@
         lax.fori_loop(first, last, body, 0)
 
     each(1, n, lambda step: meta_copy(step).start())
-    early = min(EARLY, n - 1) + 1
-    each(1, early, lambda step: new_copy(step).start())
-    loads[2].wait()
-    loads[3].wait()
-    each(1, n, lambda step: arrival(step, recv_meta, meta_recv_sem).wait())
-    table_copy = pltpu.make_async_copy(recv_meta, tables, table_sem)
-    table_copy.start()
-    table_copy.wait()
-
-    def fill_pre(target):
-        slot = jnp.int32(0)
+
+    def wanted(conversation, holder):
+        slot = jnp.int32(-1)
         for j in range(prefix_pages):
             slot = jnp.where(
-                tables[target, 0, new_pages + j] == me,
-                tables[target, 0, SLOT_LANE + new_pages + j],
+                tables[conversation, 0, new_pages + j] == holder,
+                tables[conversation, 0, SLOT_LANE + new_pages + j],
                 slot,
             )
-        for side in range(2):
-            send_pre[target, side] = pool[side, slot]
-
-    def ask(step):
-        fill_pre(peer(step))
-
-    ask(1)
-
-    def pipelined(step):
-        ask(step)
-        pre_copy(step - 1).start()
-
-    each(2, n, pipelined)
-    fill_pre(me)
-    pre_copy(n - 1).start()
-    recv_pre[me] = send_pre[me]
-    each(early, n, lambda step: new_copy(step).start())
-
-    def clear(slot):
-        source[slot] = -1
-
-    each(0, slots, clear)
-
-    def incoming(device, carry):
-        landing = jnp.int32(-1)
-        for i in range(new_pages):
-            landing = jnp.where(
-                tables[device, 0, i] == me, tables[device, 0, SLOT_LANE + i], landing
-            )
-
-        for slot in range(slots):
-            source[slot] = jnp.where(landing == slot, device, source[slot])
-        return carry
-
-    lax.fori_loop(0, n, incoming, 0)
-    loads[4].wait()
-
-    each(1, n, lambda step: arrival(step, recv_pre, pre_recv_sem).wait())
-    for j in range(prefix_pages):
-        for side in range(2):
-            prefix[side, j * page_rows : (j + 1) * page_rows, :] = recv_pre[page_holder[0, j], side]
+        return slot
+
+    def read_tables():
+        each(1, n, lambda step: arrival(step, recv_meta, meta_recv_sem).wait())
+        table_copy = pltpu.make_async_copy(recv_meta, tables, table_sem)
+        table_copy.start()
+        table_copy.wait()
+
+    def index_incoming():
+        def clear(slot):
+            source[slot] = -1
+
+        each(0, slots, clear)
+
+        def incoming(device):
+            landing = jnp.int32(-1)
+            for i in range(new_pages):
+                landing = jnp.where(
+                    tables[device, 0, i] == me, tables[device, 0, SLOT_LANE + i], landing
+                )
+
+            for slot in range(slots):
+                source[slot] = jnp.where(landing == slot, device, source[slot])
+
+        each(0, n, incoming)
+
+    if halves:
+        (
+            mirror_k,
+            mirror_v,
+            mirrored_k,
+            mirrored_v,
+            send_own,
+            recv_own,
+            relay_k,
+            relay_v,
+            recv_k,
+            recv_v,
+            ranks,
+            mirror_send_sem,
+            mirror_recv_sem,
+            own_send_sem,
+            own_recv_sem,
+            relay_send_sem,
+            relay_recv_sem,
+        ) = exchange
+        half, plane = n // 2, n // 4
+        layer, place = me // plane, lax.rem(me, plane)
+        mine_half = me // half
+        base, other = mine_half * half, (1 - mine_half) * half
+        inner = (layer == 1) | (layer == 2)
+        here = me - base
+        kept = mirror_k.shape[0]
+
+        def in_layer(which, i):
+            return which * plane + lax.rem(place + i, plane)
+
+        beside = base // plane + 1 - lax.rem(layer, 2)
+        near = 2 - mine_half
+        far = 3 - 3 * mine_half
+
+        def send_layer(which, first, last):
+            each(first, last, lambda i: new_to(in_layer(which, i)).start())
+
+        send_layer(far, 0, FIRST)
+        send_layer(layer, 1, plane)
+
+        mirror_at = half - plane * mine_half + place
+        origin = lax.rem(layer, 2)
+
+        def mirror_copy(which, sent, received):
+            return remote(
+                sent,
+                received.at[origin],
+                mirror_send_sem.at[which],
+                mirror_recv_sem.at[origin, which],
+                mirror_at,
+            )
+
+        def half_peer(i):
+            return lax.rem(here + i, half)
+
+        def own_copy(i):
+            to = half_peer(i)
+            return remote(
+                send_own.at[to],
+                recv_own.at[here],
+                own_send_sem.at[to],
+                own_recv_sem.at[here],
+                base + to,
+            )
+
+        def relay_copy(i, which):
+            to = half_peer(i)
+            sent, received = ((relay_k, recv_k), (relay_v, recv_v))[which]
+            return remote(
+                sent.at[to],
+                received.at[place],
+                relay_send_sem.at[to, which],
+                relay_recv_sem.at[place, which],
+                base + to,
+            )
+
+        loads[2].wait()
+        loads[3].wait()
+        read_tables()
+
+        def pick(i, carry):
+            count, picks = carry
+            slot = wanted(other + i, me)
+            found = slot >= 0
+            picks = tuple(
+                jnp.where(found & (count == k), slot, p) for k, p in enumerate(picks)
+            )
+            return count + jnp.where(found, 1, 0), picks
+
+        picks = lax.fori_loop(
+            0, half, pick, (jnp.int32(0), (jnp.int32(0),) * kept)
+        )[1]
+        for k in range(kept):
+            mirror_k[k] = pool[0, picks[k]]
+        for k in range(kept):
+            mirror_v[k] = pool[1, picks[k]]
+        mirror_copy(0, mirror_k, mirrored_k).start()
+        mirror_copy(1, mirror_v, mirrored_v).start()
+
+        def fill_own(i):
+            to = half_peer(i)
+            slot = jnp.maximum(wanted(base + to, me), 0)
+            for side in range(2):
+                send_own[to, side] = pool[side, slot]
+
+        fill_own(1)
+
+        def own_step(i):
+            fill_own(i)
+            own_copy(i - 1).start()
+
+        each(2, half, own_step)
+        fill_own(0)
+        own_copy(half - 1).start()
+        recv_own[here] = send_own[here]
+
+        send_layer(beside, 0, plane)
+        send_layer(near, 0, plane)
+
+        @pl.when(inner)
+        def _():
+            for o in range(2):
+                def rank(i, count):
+                    ranks[i * 2 + o] = jnp.minimum(count, kept - 1)
+                    found = wanted(base + i, other + o * plane + place) >= 0
+                    return count + jnp.where(found, 1, 0)
+
+                lax.fori_loop(0, half, rank, jnp.int32(0))
+
+            for which in range(2):
+                sent, got = ((relay_k, mirrored_k), (relay_v, mirrored_v))[which]
+                received = (recv_k, recv_v)[which]
+                for o in range(2):
+                    landed(got.at[o], mirror_recv_sem.at[o, which]).wait()
+
+                def fill_relay(i):
+                    to = half_peer(i)
+                    for o in range(2):
+                        sent[to, o] = got[o, ranks[to * 2 + o]]
+
+                fill_relay(1)
+
+                def relay_step(i):
+                    fill_relay(i)
+                    relay_copy(i - 1, which).start()
+
+                each(2, half, relay_step)
+                fill_relay(0)
+                relay_copy(half - 1, which).start()
+                received[place] = sent[here]
+            send_layer(far, FIRST, plane)
+
+        index_incoming()
+        loads[4].wait()
+
+        each(1, half, lambda i: landed(
+            recv_own.at[half_peer(i)], own_recv_sem.at[half_peer(i)]
+        ).wait())
+        for which in range(2):
+            received = (recv_k, recv_v)[which]
+
+            def relayed(i):
+                @pl.when(jnp.logical_not(inner & (i == place)))
+                def _():
+                    landed(received.at[i], relay_recv_sem.at[i, which]).wait()
+
+            each(0, plane, relayed)
+
+        @pl.when(jnp.logical_not(inner))
+        def _():
+            send_layer(far, FIRST, plane)
+
+        for j in range(prefix_pages):
+            holder = page_holder[0, j]
+            close = holder // half == mine_half
+            for side in range(2):
+                own = recv_own[lax.rem(holder, half), side]
+                through = (recv_k, recv_v)[side][
+                    lax.rem(holder, plane), lax.rem(holder // plane, 2)
+                ]
+                prefix[side, j * page_rows : (j + 1) * page_rows, :] = jnp.where(
+                    close, own, through
+                )
+
+        def sent_pages():
+            mirror_copy(0, mirror_k, mirrored_k).wait_send()
+            mirror_copy(1, mirror_v, mirrored_v).wait_send()
+            each(1, half, lambda i: own_copy(i).wait_send())
+
+            @pl.when(inner)
+            def _():
+                for which in range(2):
+                    each(1, half, lambda i: relay_copy(i, which).wait_send())
+
+    else:
+        send_pre, recv_pre, pre_send_sem, pre_recv_sem = exchange
+
+        def pre_copy(step):
+            return remote(
+                send_pre.at[peer(step)],
+                recv_pre.at[me],
+                pre_send_sem.at[step],
+                pre_recv_sem.at[me],
+                peer(step),
+            )
+
+        early = min(EARLY, n - 1) + 1
+        each(1, early, lambda step: new_to(peer(step)).start())
+        loads[2].wait()
+        loads[3].wait()
+        read_tables()
+
+        def fill_pre(target):
+            slot = jnp.maximum(wanted(target, me), 0)
+            for side in range(2):
+                send_pre[target, side] = pool[side, slot]
+
+        fill_pre(peer(1))
+
+        def pipelined(step):
+            fill_pre(peer(step))
+            pre_copy(step - 1).start()
+
+        each(2, n, pipelined)
+        fill_pre(me)
+        pre_copy(n - 1).start()
+        recv_pre[me] = send_pre[me]
+        each(early, n, lambda step: new_to(peer(step)).start())
+        index_incoming()
+        loads[4].wait()
+
+        each(1, n, lambda step: arrival(step, recv_pre, pre_recv_sem).wait())
+        for j in range(prefix_pages):
+            for side in range(2):
+                prefix[side, j * page_rows : (j + 1) * page_rows, :] = recv_pre[
+                    page_holder[0, j], side
+                ]
+
+        def sent_pages():
+            each(1, n, lambda step: pre_copy(step).wait_send())
 
     factor = math.log2(math.e) / math.sqrt(HEAD)
     nt = (((1,), (1,)), ((), ()))
@@ -270,8 +492,8 @@
 
     each(1, n, lambda step: arrival(step, recv_new, new_recv_sem).wait())
     each(1, n, lambda step: meta_copy(step).wait_send())
-    each(1, n, lambda step: new_copy(step).wait_send())
-    each(1, n, lambda step: pre_copy(step).wait_send())
+    each(1, n, lambda step: new_to(peer(step)).wait_send())
+    sent_pages()
 
 
 def finish(source, out, recv_new, pool, o_hbm, pko_hbm, pvo_hbm, pool_out, sem):
@@ -322,8 +544,34 @@
     kind = queries.dtype
     smem = pl.BlockSpec(memory_space=pltpu.SMEM)
     anywhere = pl.BlockSpec(memory_space=pl.ANY)
-    exchange = pltpu.VMEM((n, 2, page_rows, width), kind)
     peers = pltpu.SemaphoreType.DMA((n,))
+
+    def pages(*count):
+        return pltpu.VMEM((*count, page_rows, width), kind)
+
+    if crosses_once(n, new_pages):
+        half, plane, left = n // 2, n // 4, slots - new_pages
+        exchange = [
+            pages(left),
+            pages(left),
+            pages(2, left),
+            pages(2, left),
+            pages(half, 2),
+            pages(half, 2),
+            pages(half, 2),
+            pages(half, 2),
+            pages(plane, 2),
+            pages(plane, 2),
+            pltpu.SMEM((n,), jnp.int32),
+            pltpu.SemaphoreType.DMA((2,)),
+            pltpu.SemaphoreType.DMA((2, 2)),
+            pltpu.SemaphoreType.DMA((half,)),
+            pltpu.SemaphoreType.DMA((half,)),
+            pltpu.SemaphoreType.DMA((half, 2)),
+            pltpu.SemaphoreType.DMA((plane, 2)),
+        ]
+    else:
+        exchange = [pages(n, 2), pages(n, 2), peers, peers]
     held = pl.BlockSpec(memory_space=pltpu.VMEM)
     page_bytes = 2 * page_rows * width * kind.itemsize
     kept = queries.size * kind.itemsize + (n + slots) * page_bytes
@@ -347,9 +595,7 @@
             pltpu.VMEM(queries.shape, kind),
             pltpu.VMEM((2, span // page_rows, page_rows, width), kind),
             pltpu.VMEM((2, padded, width), kind),
-            exchange,
-            exchange,
-            exchange,
+            pages(n, 2),
             pltpu.VMEM((1, 128), jnp.int32),
             pltpu.VMEM((n, 1, 128), jnp.int32),
             pltpu.SMEM((n, 1, 128), jnp.int32),
@@ -359,8 +605,7 @@
             peers,
             peers,
             peers,
-            peers,
-            peers,
+            *exchange,
         ],
         compiler_params=pltpu.CompilerParams(
             collective_id=0, has_side_effects=True, vmem_limit_bytes=grant

time: 58.9 us -> 53.9 us (0.915)
  the two profiles are of different devices: /device:TPU:11 before, /device:TPU:1 now
where the time goes in v1:
time: 53.9 us; the launch traced here: 53.7 us
  Pallas kernels  51.1 us (95%)
  between operations  1.94 us (4%)
  local copies, waits for them, and re-layouts  0.62 us (1%)
    pallas_call x1, Pallas kernels, shards(): pl.pallas_call(functools.partial(kernel, n, new_pages, prefix_pages), out...  48.8 us
    pallas_call x1, Pallas kernels, shards(): pl.pallas_call(finish, out_shape=results, in_specs=[smem, held, held, hel...  2.33 us

profile of v1, /device:TPU:1, one launch (start us, length us, event | category | flops | bytes accessed | tf_op | source)
XLA Modules:
  0.0 53.7 jit_solution(5358794066274762295)
XLA Ops:
  1.9 48.8 %shard_map.130 = (bf16[256,4096]{1,0:T(8,128)(2,1)S(1)}, bf16[16,2,16,1024]{3,2,1,0:T(8,128)(2,1)S(1)}, bf16[2,21,16,1024]{3,2,1,0:T(8,128)(2,1)S(1)}, s32[21]{0:T(128)}) custom-call(s32[1]{0:T(128)S(6)} %copy.14.prefix_len, s32[1]{0:T(128)S(6)} %copy.15.new_len, s32[1,5]{1,0:T(1,128)} %page_holder.1, s32[1,5]{1,0:T(1,128)} %page_slot.1, ...), custom_call_target="tpu_custom_call" | custom-call | tf_op jit(solution)/shard_map/pallas_call | solution.py:584
  50.7 0.0 copy-start
  50.7 0.6 %copy-done = s32[21]{0:T(128)S(1)} copy-done((s32[21]{0:T(128)S(1)}, s32[21]{0:T(128)}, u32[]{:S(2)}) %copy-start) | copy-done | bytes 108
  51.3 2.3 %shard_map.131 = (bf16[256,4096]{1,0:T(8,128)(2,1)}, bf16[21,16,1024]{2,1,0:T(8,128)(2,1)}, bf16[21,16,1024]{2,1,0:T(8,128)(2,1)}) custom-call(s32[21]{0:T(128)S(1)} %copy-done, bf16[256,4096]{1,0:T(8,128)(2,1)S(1)} %get-tuple-element.8.out, bf16[16,2,16,1024]{3,2,1,0:T(8,128)(2,1)S(1)} %get-tuple-element.9.recv_new, ...), custom_call_target="tpu_custom_call" | custom-call | tf_op jit(solution)/shard_map/pallas_call | solution.py:626
Async XLA Ops:
  50.7 0.6 %copy-start = (s32[21]{0:T(128)S(1)}, s32[21]{0:T(128)}, u32[]{:S(2)}) copy-start(s32[21]{0:T(128)} %get-tuple-element.7.source) | copy-start | bytes 256

commit v2 on v1

--- a/solution.py
+++ b/solution.py
@@ -14,7 +14,7 @@
 ROWS = 128
 SLOT_LANE = 64
 EARLY = 5
-FIRST = 1
+FIRST = 2
 MESH = pl.DeviceIdType.MESH
 
 
@@ -26,21 +26,28 @@
     n,
     new_pages,
     prefix_pages,
+    prefix_len_hbm,
+    new_len_hbm,
+    page_holder_hbm,
+    page_slot_hbm,
+    new_holder_hbm,
+    new_slot_hbm,
+    q_hbm,
+    k_hbm,
+    v_hbm,
+    pk_hbm,
+    pv_hbm,
+    out,
+    pool_out,
+    recv_new,
+    pool,
+    source,
     prefix_len,
     new_len,
     page_holder,
     page_slot,
     new_holder,
     new_slot,
-    q_hbm,
-    k_hbm,
-    v_hbm,
-    pk_hbm,
-    pv_hbm,
-    out,
-    recv_new,
-    pool,
-    source,
     q,
     kv,
     prefix,
@@ -49,6 +56,7 @@
     recv_meta,
     tables,
     in_sem,
+    own_sem,
     table_sem,
     meta_send_sem,
     meta_recv_sem,
@@ -64,6 +72,32 @@
     slots = pool.shape[1]
     group = HEADS // KV_HEADS
 
+    def peer(step):
+        return lax.rem(me + step, n)
+
+    barrier = pltpu.get_barrier_semaphore()
+
+    def greet(step, carry):
+        pl.semaphore_signal(barrier, inc=1, device_id=(mine, peer(step)), device_id_type=MESH)
+        return carry
+
+    lax.fori_loop(1, n, greet, 0)
+
+    given = [
+        pltpu.make_async_copy(there, here, own_sem.at[i])
+        for i, (there, here) in enumerate(
+            (
+                (new_holder_hbm, new_holder),
+                (new_slot_hbm, new_slot),
+                (page_holder_hbm, page_holder),
+                (page_slot_hbm, page_slot),
+                (new_len_hbm, new_len),
+                (prefix_len_hbm, prefix_len),
+            )
+        )
+    ]
+    for copy in given:
+        copy.start()
     loads = [
         pltpu.make_async_copy(k_hbm, kv.at[0], in_sem.at[0]),
         pltpu.make_async_copy(v_hbm, kv.at[1], in_sem.at[1]),
@@ -74,16 +108,8 @@
     for load in loads:
         load.start()
 
-    def peer(step):
-        return lax.rem(me + step, n)
-
-    barrier = pltpu.get_barrier_semaphore()
-
-    def greet(step, carry):
-        pl.semaphore_signal(barrier, inc=1, device_id=(mine, peer(step)), device_id_type=MESH)
-        return carry
-
-    lax.fori_loop(1, n, greet, 0)
+    for copy in given:
+        copy.wait()
 
     lanes = lax.broadcasted_iota(jnp.int32, meta.shape, 1)
     row = jnp.full(meta.shape, -1, jnp.int32)
@@ -96,13 +122,10 @@
     meta[...] = row
     recv_meta[me] = row
 
-    prefix[...] = jnp.zeros_like(prefix)
     live = new_len[0]
-    loads[0].wait()
-    loads[1].wait()
     page_pos = lax.broadcasted_iota(jnp.int32, (page_rows, kv.shape[3]), 0)
 
-    def fill_new(target, carry):
+    def fill_new(target):
         page = jnp.int32(0)
         for i in range(new_pages):
             page = jnp.where(new_holder[0, i] == target, i, page)
@@ -110,10 +133,6 @@
         for side in range(2):
             rows = kv[side, page]
             send_new[target, side] = jnp.where(keep, rows, jnp.zeros_like(rows))
-        return carry
-
-    lax.fori_loop(0, n, fill_new, 0)
-    recv_new[me] = send_new[me]
 
     def remote(sent, received, send_sem, recv_sem, target):
         return pltpu.make_async_remote_copy(
@@ -156,6 +175,8 @@
         lax.fori_loop(first, last, body, 0)
 
     each(1, n, lambda step: meta_copy(step).start())
+    loads[0].wait()
+    loads[1].wait()
 
     def wanted(conversation, holder):
         slot = jnp.int32(-1)
@@ -229,8 +250,19 @@
         def send_layer(which, first, last):
             each(first, last, lambda i: new_to(in_layer(which, i)).start())
 
+        def fill_layer(which, first, last):
+            each(first, last, lambda i: fill_new(in_layer(which, i)))
+
+        fill_layer(far, 0, FIRST)
+        fill_layer(layer, 1, plane)
         send_layer(far, 0, FIRST)
+        fill_layer(layer, 0, 1)
         send_layer(layer, 1, plane)
+        recv_new[me] = send_new[me]
+        fill_layer(beside, 0, plane)
+        fill_layer(near, 0, plane)
+        fill_layer(far, FIRST, plane)
+        prefix[...] = jnp.zeros_like(prefix)
 
         mirror_at = half - plane * mine_half + place
         origin = lax.rem(layer, 2)
@@ -398,6 +430,9 @@
                 peer(step),
             )
 
+        each(0, n, fill_new)
+        recv_new[me] = send_new[me]
+        prefix[...] = jnp.zeros_like(prefix)
         early = min(EARLY, n - 1) + 1
         each(1, early, lambda step: new_to(peer(step)).start())
         loads[2].wait()
@@ -491,35 +526,30 @@
     each(0, KV_HEADS, attend)
 
     each(1, n, lambda step: arrival(step, recv_new, new_recv_sem).wait())
+
+    def place_page(slot):
+        device = source[slot]
+        for side in range(2):
+            pool_out[side, slot] = jnp.where(
+                device >= 0, recv_new[jnp.maximum(device, 0), side], pool[side, slot]
+            )
+
+    each(0, slots, place_page)
     each(1, n, lambda step: meta_copy(step).wait_send())
     each(1, n, lambda step: new_to(peer(step)).wait_send())
     sent_pages()
 
 
-def finish(source, out, recv_new, pool, o_hbm, pko_hbm, pvo_hbm, pool_out, sem):
-    slots = pool.shape[1]
-    whole = pltpu.make_async_copy(out, o_hbm, sem.at[0])
-    whole.start()
-
-    def place(slot, carry):
-        device = source[slot]
-        found = device >= 0
-        for side in range(2):
-            pool_out[side, slot] = jnp.where(
-                found, recv_new[jnp.maximum(device, 0), side], pool[side, slot]
-            )
-        return carry
-
-    lax.fori_loop(0, slots, place, 0)
+def finish(out, pool_out, o_hbm, pko_hbm, pvo_hbm, sem):
     stores = [
         pltpu.make_async_copy(pool_out.at[0], pko_hbm, sem.at[1]),
         pltpu.make_async_copy(pool_out.at[1], pvo_hbm, sem.at[2]),
+        pltpu.make_async_copy(out, o_hbm, sem.at[0]),
     ]
     for store in stores:
         store.start()
     for store in stores:
         store.wait()
-    whole.wait()
 
 
 def shards(
@@ -542,7 +572,7 @@
     prefix_pages = page_holder.shape[1]
     padded = -(-prefix_pages * page_rows // ROWS) * ROWS
     kind = queries.dtype
-    smem = pl.BlockSpec(memory_space=pltpu.SMEM)
+    tables = (prefix_len, new_len, page_holder, page_slot, new_holder, new_slot)
     anywhere = pl.BlockSpec(memory_space=pl.ANY)
     peers = pltpu.SemaphoreType.DMA((n,))
 
@@ -574,24 +604,26 @@
         exchange = [pages(n, 2), pages(n, 2), peers, peers]
     held = pl.BlockSpec(memory_space=pltpu.VMEM)
     page_bytes = 2 * page_rows * width * kind.itemsize
-    kept = queries.size * kind.itemsize + (n + slots) * page_bytes
+    kept = queries.size * kind.itemsize + slots * page_bytes
     grant = 67043328 - kept - 256 * 1024
     results = (
         jax.ShapeDtypeStruct(queries.shape, kind),
         jax.ShapeDtypeStruct(pool_keys.shape, kind),
         jax.ShapeDtypeStruct(pool_values.shape, kind),
     )
-    out, recv_new, pool, source = pl.pallas_call(
+    out, pool_out = pl.pallas_call(
         functools.partial(kernel, n, new_pages, prefix_pages),
         out_shape=(
             pltpu.VMEM(queries.shape, kind),
-            pltpu.VMEM((n, 2, page_rows, width), kind),
             pltpu.VMEM((2, slots, page_rows, width), kind),
-            jax.ShapeDtypeStruct((slots,), jnp.int32),
         ),
-        in_specs=[smem] * 6 + [anywhere] * 5,
-        out_specs=(held, held, held, smem),
+        in_specs=[anywhere] * 11,
+        out_specs=(held, held),
         scratch_shapes=[
+            pages(n, 2),
+            pages(2, slots),
+            pltpu.SMEM((slots,), jnp.int32),
+            *[pltpu.SMEM(table.shape, table.dtype) for table in tables],
             pltpu.VMEM(queries.shape, kind),
             pltpu.VMEM((2, span // page_rows, page_rows, width), kind),
             pltpu.VMEM((2, padded, width), kind),
@@ -600,6 +632,7 @@
             pltpu.VMEM((n, 1, 128), jnp.int32),
             pltpu.SMEM((n, 1, 128), jnp.int32),
             pltpu.SemaphoreType.DMA((5,)),
+            pltpu.SemaphoreType.DMA((len(tables),)),
             pltpu.SemaphoreType.DMA,
             peers,
             peers,
@@ -611,12 +644,7 @@
             collective_id=0, has_side_effects=True, vmem_limit_bytes=grant
         ),
     )(
-        prefix_len,
-        new_len,
-        page_holder,
-        page_slot,
-        new_holder,
-        new_slot,
+        *tables,
         queries,
         new_keys.reshape(span // page_rows, page_rows, width),
         new_values.reshape(span // page_rows, page_rows, width),
@@ -626,16 +654,11 @@
     return pl.pallas_call(
         finish,
         out_shape=results,
-        in_specs=[smem, held, held, held],
+        in_specs=[held, held],
         out_specs=(anywhere,) * 3,
-        scratch_shapes=[
-            pltpu.VMEM((2, slots, page_rows, width), kind),
-            pltpu.SemaphoreType.DMA((3,)),
-        ],
-        compiler_params=pltpu.CompilerParams(
-            vmem_limit_bytes=slots * page_bytes + 4 * 1024 * 1024
-        ),
-    )(source, out, recv_new, pool)
+        scratch_shapes=[pltpu.SemaphoreType.DMA((3,))],
+        compiler_params=pltpu.CompilerParams(vmem_limit_bytes=1024 * 1024),
+    )(out, pool_out)
 
 
 def solution(mesh):

time: 53.9 us -> 49.9 us (0.926)
  Pallas kernels: 51.1 us -> 47.4 us
  local copies, waits for them, and re-layouts: 0.62 us -> 0 us
    pallas_call x1, Pallas kernels: 48.8 us -> 45.6 us  [shards(): pl.pallas_call(functools.partial(kernel, n, new_pages, prefix_pages), out...]
    unnamed x2 -> x0, local copies, waits for them, and re-layouts: 0.62 us -> none
where the time goes in v2:
time: 49.9 us; the launch traced here: 49.3 us
  Pallas kernels  47.4 us (95%)
  between operations  1.93 us (4%)
    pallas_call x1, Pallas kernels, shards(): pl.pallas_call(functools.partial(kernel, n, new_pages, prefix_pages), out...  45.6 us
    pallas_call x1, Pallas kernels, shards(): pl.pallas_call(finish, out_shape=results, in_specs=[held, held], out_spec...  1.8 us

profile of v2, /device:TPU:1, one launch (start us, length us, event | category | flops | bytes accessed | tf_op | source)
XLA Modules:
  0.0 49.3 jit_solution(17789620567103850213)
XLA Ops:
  1.9 45.6 %shard_map.130 = (bf16[256,4096]{1,0:T(8,128)(2,1)S(1)}, bf16[2,21,16,1024]{3,2,1,0:T(8,128)(2,1)S(1)}) custom-call(s32[1]{0:T(128)S(6)} %copy.14.prefix_len_hbm, s32[1]{0:T(128)S(6)} %copy.15.new_len_hbm, s32[1,5]{1,0:T(1,128)} %page_holder_hbm.1, s32[1,5]{1,0:T(1,128)} %page_slot_hbm.1, s32[1,16]{1,0:T(1,128)} %new_holder_hbm.1, s32[1,16]{1,0:T(1,128)} %new_slot_hbm.1, ...), custom_call_target="tpu_custom_call" | custom-call | tf_op jit(solution)/shard_map/pallas_call | solution.py:614
  47.5 1.8 %shard_map.131 = (bf16[256,4096]{1,0:T(8,128)(2,1)}, bf16[21,16,1024]{2,1,0:T(8,128)(2,1)}, bf16[21,16,1024]{2,1,0:T(8,128)(2,1)}) custom-call(bf16[256,4096]{1,0:T(8,128)(2,1)S(1)} %get-tuple-element.5.out, bf16[2,21,16,1024]{3,2,1,0:T(8,128)(2,1)S(1)} %get-tuple-element.6.pool_out), custom_call_target="tpu_custom_call" | custom-call | tf_op jit(solution)/shard_map/pallas_call | solution.py:654

commit v3 on v2

--- a/solution.py
+++ b/solution.py
@@ -14,7 +14,48 @@
 ROWS = 128
 SLOT_LANE = 64
 EARLY = 5
-FIRST = 2
+INNER = (
+    (("far", 0), ("far", 1)),
+    (
+        ("beside", 3),
+        ("own", 0),
+        ("mirror", 0),
+        ("layer", 1),
+        ("layer", 2),
+        ("layer", 3),
+        ("beside", 1),
+        ("far", 2),
+        ("mirror", 1),
+        ("near", 1),
+        ("near", 2),
+        ("far", 3),
+        ("beside", 2),
+        ("relay", 0),
+        ("relay", 1),
+        ("near", 3),
+    ),
+    (("beside", 0), ("near", 0)),
+)
+OUTER = (
+    (("beside", 2), ("far", 1), ("far", 2)),
+    (
+        ("own", 0),
+        ("mirror", 0),
+        ("mirror", 1),
+        ("beside", 0),
+        ("beside", 3),
+        ("beside", 1),
+        ("near", 0),
+        ("near", 3),
+        ("near", 1),
+        ("near", 2),
+        ("far", 3),
+        ("layer", 1),
+        ("layer", 2),
+        ("layer", 3),
+    ),
+    (("far", 0),),
+)
 MESH = pl.DeviceIdType.MESH
 
 
@@ -243,31 +284,45 @@
         def in_layer(which, i):
             return which * plane + lax.rem(place + i, plane)
 
-        beside = base // plane + 1 - lax.rem(layer, 2)
-        near = 2 - mine_half
-        far = 3 - 3 * mine_half
-
-        def send_layer(which, first, last):
-            each(first, last, lambda i: new_to(in_layer(which, i)).start())
-
-        def fill_layer(which, first, last):
-            each(first, last, lambda i: fill_new(in_layer(which, i)))
-
-        fill_layer(far, 0, FIRST)
-        fill_layer(layer, 1, plane)
-        send_layer(far, 0, FIRST)
-        fill_layer(layer, 0, 1)
-        send_layer(layer, 1, plane)
-        recv_new[me] = send_new[me]
-        fill_layer(beside, 0, plane)
-        fill_layer(near, 0, plane)
-        fill_layer(far, FIRST, plane)
-        prefix[...] = jnp.zeros_like(prefix)
+        layers = {
+            "layer": layer,
+            "beside": base // plane + 1 - lax.rem(layer, 2),
+            "near": 2 - mine_half,
+            "far": 3 - 3 * mine_half,
+        }
+
+        def target(which, i):
+            return in_layer(layers[which], i)
+
+        def early_fill(order):
+            for which, i in order[0]:
+                fill_new(target(which, i))
+
+        def late_fill(order):
+            for which, i in order[1] + order[2]:
+                if which in layers:
+                    fill_new(target(which, i))
+
+        def stage(order, number):
+            for which, i in order[number]:
+                if which == "own":
+                    each(1, half, lambda j: own_copy(j).start())
+                elif which == "mirror":
+                    mirror_copy(i).start()
+                elif which == "relay":
+                    forward(i)
+                else:
+                    new_to(target(which, i)).start()
+
+        def by_layer(act):
+            pl.when(inner)(functools.partial(act, INNER))
+            pl.when(jnp.logical_not(inner))(functools.partial(act, OUTER))
 
         mirror_at = half - plane * mine_half + place
         origin = lax.rem(layer, 2)
 
-        def mirror_copy(which, sent, received):
+        def mirror_copy(which):
+            sent, received = ((mirror_k, mirrored_k), (mirror_v, mirrored_v))[which]
             return remote(
                 sent,
                 received.at[origin],
@@ -300,6 +355,34 @@
                 base + to,
             )
 
+        def forward(which):
+            sent, got = ((relay_k, mirrored_k), (relay_v, mirrored_v))[which]
+            received = (recv_k, recv_v)[which]
+            for o in range(2):
+                landed(got.at[o], mirror_recv_sem.at[o, which]).wait()
+
+            def fill_relay(i):
+                to = half_peer(i)
+                for o in range(2):
+                    sent[to, o] = got[o, ranks[to * 2 + o]]
+
+            fill_relay(1)
+
+            def relay_step(i):
+                fill_relay(i)
+                relay_copy(i - 1, which).start()
+
+            each(2, half, relay_step)
+            fill_relay(0)
+            relay_copy(half - 1, which).start()
+            received[place] = sent[here]
+
+        by_layer(early_fill)
+        by_layer(lambda order: stage(order, 0))
+        by_layer(late_fill)
+        fill_new(me)
+        recv_new[me] = send_new[me]
+        prefix[...] = jnp.zeros_like(prefix)
         loads[2].wait()
         loads[3].wait()
         read_tables()
@@ -320,62 +403,24 @@
             mirror_k[k] = pool[0, picks[k]]
         for k in range(kept):
             mirror_v[k] = pool[1, picks[k]]
-        mirror_copy(0, mirror_k, mirrored_k).start()
-        mirror_copy(1, mirror_v, mirrored_v).start()
-
-        def fill_own(i):
-            to = half_peer(i)
+
+        def fill_own(to):
             slot = jnp.maximum(wanted(base + to, me), 0)
             for side in range(2):
                 send_own[to, side] = pool[side, slot]
 
-        fill_own(1)
-
-        def own_step(i):
-            fill_own(i)
-            own_copy(i - 1).start()
-
-        each(2, half, own_step)
-        fill_own(0)
-        own_copy(half - 1).start()
+        each(0, half, fill_own)
+
+        for o in range(2):
+            def rank(i, count):
+                ranks[i * 2 + o] = jnp.minimum(count, kept - 1)
+                found = wanted(base + i, other + o * plane + place) >= 0
+                return count + jnp.where(found, 1, 0)
+
+            lax.fori_loop(0, half, rank, jnp.int32(0))
+
+        by_layer(lambda order: stage(order, 1))
         recv_own[here] = send_own[here]
-
-        send_layer(beside, 0, plane)
-        send_layer(near, 0, plane)
-
-        @pl.when(inner)
-        def _():
-            for o in range(2):
-                def rank(i, count):
-                    ranks[i * 2 + o] = jnp.minimum(count, kept - 1)
-                    found = wanted(base + i, other + o * plane + place) >= 0
-                    return count + jnp.where(found, 1, 0)
-
-                lax.fori_loop(0, half, rank, jnp.int32(0))
-
-            for which in range(2):
-                sent, got = ((relay_k, mirrored_k), (relay_v, mirrored_v))[which]
-                received = (recv_k, recv_v)[which]
-                for o in range(2):
-                    landed(got.at[o], mirror_recv_sem.at[o, which]).wait()
-
-                def fill_relay(i):
-                    to = half_peer(i)
-                    for o in range(2):
-                        sent[to, o] = got[o, ranks[to * 2 + o]]
-
-                fill_relay(1)
-
-                def relay_step(i):
-                    fill_relay(i)
-                    relay_copy(i - 1, which).start()
-
-                each(2, half, relay_step)
-                fill_relay(0)
-                relay_copy(half - 1, which).start()
-                received[place] = sent[here]
-            send_layer(far, FIRST, plane)
-
         index_incoming()
         loads[4].wait()
 
@@ -392,9 +437,7 @@
 
             each(0, plane, relayed)
 
-        @pl.when(jnp.logical_not(inner))
-        def _():
-            send_layer(far, FIRST, plane)
+        by_layer(lambda order: stage(order, 2))
 
         for j in range(prefix_pages):
             holder = page_holder[0, j]
@@ -409,8 +452,8 @@
                 )
 
         def sent_pages():
-            mirror_copy(0, mirror_k, mirrored_k).wait_send()
-            mirror_copy(1, mirror_v, mirrored_v).wait_send()
+            mirror_copy(0).wait_send()
+            mirror_copy(1).wait_send()
             each(1, half, lambda i: own_copy(i).wait_send())
 
             @pl.when(inner)

time: 49.9 us -> 47.9 us (0.960)
  the two profiles are of different devices: /device:TPU:1 before, /device:TPU:27 now
where the time goes in v3:
time: 47.9 us; the launch traced here: 47.7 us
  Pallas kernels  45.8 us (96%)
  between operations  1.93 us (4%)
    pallas_call x1, Pallas kernels, shards(): pl.pallas_call(functools.partial(kernel, n, new_pages, prefix_pages), out...  44 us
    pallas_call x1, Pallas kernels, shards(): pl.pallas_call(finish, out_shape=results, in_specs=[held, held], out_spec...  1.8 us

profile of v3, /device:TPU:27, one launch (start us, length us, event | category | flops | bytes accessed | tf_op | source)
XLA Modules:
  0.0 47.7 jit_solution(17018155248405740377)
XLA Ops:
  1.9 44.0 %shard_map.130 = (bf16[256,4096]{1,0:T(8,128)(2,1)S(1)}, bf16[2,21,16,1024]{3,2,1,0:T(8,128)(2,1)S(1)}) custom-call(s32[1]{0:T(128)S(6)} %copy.14.prefix_len_hbm, s32[1]{0:T(128)S(6)} %copy.15.new_len_hbm, s32[1,5]{1,0:T(1,128)} %page_holder_hbm.1, s32[1,5]{1,0:T(1,128)} %page_slot_hbm.1, s32[1,16]{1,0:T(1,128)} %new_holder_hbm.1, s32[1,16]{1,0:T(1,128)} %new_slot_hbm.1, ...), custom_call_target="tpu_custom_call" | custom-call | tf_op jit(solution)/shard_map/pallas_call | solution.py:657
  45.9 1.8 %shard_map.131 = (bf16[256,4096]{1,0:T(8,128)(2,1)}, bf16[21,16,1024]{2,1,0:T(8,128)(2,1)}, bf16[21,16,1024]{2,1,0:T(8,128)(2,1)}) custom-call(bf16[256,4096]{1,0:T(8,128)(2,1)S(1)} %get-tuple-element.5.out, bf16[2,21,16,1024]{3,2,1,0:T(8,128)(2,1)S(1)} %get-tuple-element.6.pool_out), custom_call_target="tpu_custom_call" | custom-call | tf_op jit(solution)/shard_map/pallas_call | solution.py:697

commit v4 on v3

--- a/solution.py
+++ b/solution.py
@@ -79,7 +79,6 @@
     pk_hbm,
     pv_hbm,
     out,
-    pool_out,
     recv_new,
     pool,
     source,
@@ -236,22 +235,15 @@
         table_copy.wait()
 
     def index_incoming():
-        def clear(slot):
-            source[slot] = -1
-
-        each(0, slots, clear)
-
-        def incoming(device):
+        def incoming(device, origins):
             landing = jnp.int32(-1)
             for i in range(new_pages):
                 landing = jnp.where(
                     tables[device, 0, i] == me, tables[device, 0, SLOT_LANE + i], landing
                 )
-
-            for slot in range(slots):
-                source[slot] = jnp.where(landing == slot, device, source[slot])
-
-        each(0, n, incoming)
+            return jnp.where(lanes == landing, device, origins)
+
+        source[...] = lax.fori_loop(0, n, incoming, jnp.full(source.shape, -1, jnp.int32))
 
     if halves:
         (
@@ -332,7 +324,10 @@
             )
 
         def half_peer(i):
-            return lax.rem(here + i, half)
+            away = (i > 0) & (i <= plane)
+            which = jnp.where(away, layers["beside"], layer)
+            turn = place + jnp.where(away, i - 1, i)
+            return which * plane + lax.rem(turn, plane) - base
 
         def own_copy(i):
             to = half_peer(i)
@@ -569,30 +564,42 @@
     each(0, KV_HEADS, attend)
 
     each(1, n, lambda step: arrival(step, recv_new, new_recv_sem).wait())
-
-    def place_page(slot):
-        device = source[slot]
-        for side in range(2):
-            pool_out[side, slot] = jnp.where(
-                device >= 0, recv_new[jnp.maximum(device, 0), side], pool[side, slot]
-            )
-
-    each(0, slots, place_page)
     each(1, n, lambda step: meta_copy(step).wait_send())
     each(1, n, lambda step: new_to(peer(step)).wait_send())
     sent_pages()
 
 
-def finish(out, pool_out, o_hbm, pko_hbm, pvo_hbm, sem):
-    stores = [
-        pltpu.make_async_copy(pool_out.at[0], pko_hbm, sem.at[1]),
-        pltpu.make_async_copy(pool_out.at[1], pvo_hbm, sem.at[2]),
-        pltpu.make_async_copy(out, o_hbm, sem.at[0]),
-    ]
-    for store in stores:
-        store.start()
-    for store in stores:
-        store.wait()
+def finish(out, recv_new, pool, source, o_hbm, pko_hbm, pvo_hbm, origins, origin_sem, sem):
+    table = pltpu.make_async_copy(source, origins, origin_sem)
+    table.start()
+    whole = pltpu.make_async_copy(out, o_hbm, sem.at[0])
+    whole.start()
+    table.wait()
+    targets = (pko_hbm, pvo_hbm)
+
+    def place(slot, carry):
+        device = origins[0, slot]
+
+        @pl.when(device >= 0)
+        def _():
+            for side in range(2):
+                pltpu.make_async_copy(
+                    recv_new.at[device, side], targets[side].at[slot], sem.at[1 + side]
+                ).start()
+
+        @pl.when(device < 0)
+        def _():
+            for side in range(2):
+                pltpu.make_async_copy(
+                    pool.at[side, slot], targets[side].at[slot], sem.at[1 + side]
+                ).start()
+
+        return carry
+
+    lax.fori_loop(0, pool.shape[1], place, 0)
+    for side in range(2):
+        pltpu.make_async_copy(pool.at[side], targets[side], sem.at[1 + side]).wait()
+    whole.wait()
 
 
 def shards(
@@ -647,25 +654,24 @@
         exchange = [pages(n, 2), pages(n, 2), peers, peers]
     held = pl.BlockSpec(memory_space=pltpu.VMEM)
     page_bytes = 2 * page_rows * width * kind.itemsize
-    kept = queries.size * kind.itemsize + slots * page_bytes
+    kept = queries.size * kind.itemsize + (n + slots) * page_bytes + 4096
     grant = 67043328 - kept - 256 * 1024
     results = (
         jax.ShapeDtypeStruct(queries.shape, kind),
         jax.ShapeDtypeStruct(pool_keys.shape, kind),
         jax.ShapeDtypeStruct(pool_values.shape, kind),
     )
-    out, pool_out = pl.pallas_call(
+    out, recv_new, pool, source = pl.pallas_call(
         functools.partial(kernel, n, new_pages, prefix_pages),
         out_shape=(
             pltpu.VMEM(queries.shape, kind),
-            pltpu.VMEM((2, slots, page_rows, width), kind),
+            pages(n, 2),
+            pages(2, slots),
+            pltpu.VMEM((1, 128), jnp.int32),
         ),
         in_specs=[anywhere] * 11,
-        out_specs=(held, held),
+        out_specs=(held,) * 4,
         scratch_shapes=[
-            pages(n, 2),
-            pages(2, slots),
-            pltpu.SMEM((slots,), jnp.int32),
             *[pltpu.SMEM(table.shape, table.dtype) for table in tables],
             pltpu.VMEM(queries.shape, kind),
             pltpu.VMEM((2, span // page_rows, page_rows, width), kind),
@@ -697,11 +703,15 @@
     return pl.pallas_call(
         finish,
         out_shape=results,
-        in_specs=[held, held],
+        in_specs=[held] * 4,
         out_specs=(anywhere,) * 3,
-        scratch_shapes=[pltpu.SemaphoreType.DMA((3,))],
+        scratch_shapes=[
+            pltpu.SMEM((1, 128), jnp.int32),
+            pltpu.SemaphoreType.DMA,
+            pltpu.SemaphoreType.DMA((3,)),
+        ],
         compiler_params=pltpu.CompilerParams(vmem_limit_bytes=1024 * 1024),
-    )(out, pool_out)
+    )(out, recv_new, pool, source)
 
 
 def solution(mesh):

time: 47.9 us -> 47.6 us (level)
  the two profiles are of different devices: /device:TPU:27 before, /device:TPU:1 now
where the time goes in v4:
time: 47.6 us; the launch traced here: 47.2 us
  Pallas kernels  45.2 us (95%)
  between operations  1.93 us (4%)
    pallas_call x1, Pallas kernels, shards(): pl.pallas_call(functools.partial(kernel, n, new_pages, prefix_pages), out...  43.5 us
    pallas_call x1, Pallas kernels, shards(): pl.pallas_call(finish, out_shape=results, in_specs=[held] * 4, out_specs=...  1.78 us

profile of v4, /device:TPU:1, one launch (start us, length us, event | category | flops | bytes accessed | tf_op | source)
XLA Modules:
  0.0 47.2 jit_solution(17248679072594340024)
XLA Ops:
  1.9 43.5 %shard_map.130 = (bf16[256,4096]{1,0:T(8,128)(2,1)S(1)}, bf16[16,2,16,1024]{3,2,1,0:T(8,128)(2,1)S(1)}, bf16[2,21,16,1024]{3,2,1,0:T(8,128)(2,1)S(1)}, s32[1,128]{1,0:T(1,128)S(1)}) custom-call(s32[1]{0:T(128)S(6)} %copy.14.prefix_len_hbm, s32[1]{0:T(128)S(6)} %copy.15.new_len_hbm, s32[1,5]{1,0:T(1,128)} %page_holder_hbm.1, s32[1,5]{1,0:T(1,128)} %page_slot_hbm.1, ...), custom_call_target="tpu_custom_call" | custom-call | tf_op jit(solution)/shard_map/pallas_call | solution.py:664
  45.4 1.8 %shard_map.131 = (bf16[256,4096]{1,0:T(8,128)(2,1)}, bf16[21,16,1024]{2,1,0:T(8,128)(2,1)}, bf16[21,16,1024]{2,1,0:T(8,128)(2,1)}) custom-call(bf16[256,4096]{1,0:T(8,128)(2,1)S(1)} %get-tuple-element.7.out, bf16[16,2,16,1024]{3,2,1,0:T(8,128)(2,1)S(1)} %get-tuple-element.8.recv_new, bf16[2,21,16,1024]{3,2,1,0:T(8,128)(2,1)S(1)} %get-tuple-element.9.pool, ...), custom_call_target="tpu_custom_call" | custom-call | tf_op jit(solution)/shard_map/pallas_call | solution.py:703

commit v5 on v4

--- a/solution.py
+++ b/solution.py
@@ -446,7 +446,7 @@
                     close, own, through
                 )
 
-        def sent_pages():
+        def wait_pages():
             mirror_copy(0).wait_send()
             mirror_copy(1).wait_send()
             each(1, half, lambda i: own_copy(i).wait_send())
@@ -455,6 +455,17 @@
             def _():
                 for which in range(2):
                     each(1, half, lambda i: relay_copy(i, which).wait_send())
+
+            each(1, n, lambda step: new_to(peer(step)).wait_send())
+
+            def new_from(which, i):
+                source = target(which, i)
+                landed(recv_new.at[source], new_recv_sem.at[source]).wait()
+
+            for which in layers:
+                each(1, plane, lambda i: new_from(which, i))
+            for which in ("beside", "far", "near"):
+                new_from(which, 0)
 
     else:
         send_pre, recv_pre, pre_send_sem, pre_recv_sem = exchange
@@ -503,8 +514,10 @@
                     page_holder[0, j], side
                 ]
 
-        def sent_pages():
+        def wait_pages():
             each(1, n, lambda step: pre_copy(step).wait_send())
+            each(1, n, lambda step: new_to(peer(step)).wait_send())
+            each(1, n, lambda step: arrival(step, recv_new, new_recv_sem).wait())
 
     factor = math.log2(math.e) / math.sqrt(HEAD)
     nt = (((1,), (1,)), ((), ()))
@@ -563,10 +576,8 @@
 
     each(0, KV_HEADS, attend)
 
-    each(1, n, lambda step: arrival(step, recv_new, new_recv_sem).wait())
     each(1, n, lambda step: meta_copy(step).wait_send())
-    each(1, n, lambda step: new_to(peer(step)).wait_send())
-    sent_pages()
+    wait_pages()
 
 
 def finish(out, recv_new, pool, source, o_hbm, pko_hbm, pvo_hbm, origins, origin_sem, sem):

time: 47.6 us -> 47 us (0.987)
  no operation moved by 1% of the time
where the time goes in v5:
time: 47 us; the launch traced here: 46.8 us
  Pallas kernels  44.9 us (96%)
  between operations  1.93 us (4%)
    pallas_call x1, Pallas kernels, shards(): pl.pallas_call(functools.partial(kernel, n, new_pages, prefix_pages), out...  43.1 us
    pallas_call x1, Pallas kernels, shards(): pl.pallas_call(finish, out_shape=results, in_specs=[held] * 4, out_specs=...  1.78 us

profile of v5, /device:TPU:1, one launch (start us, length us, event | category | flops | bytes accessed | tf_op | source)
XLA Modules:
  0.0 46.8 jit_solution(18318769906233168200)
XLA Ops:
  1.9 43.1 %shard_map.130 = (bf16[256,4096]{1,0:T(8,128)(2,1)S(1)}, bf16[16,2,16,1024]{3,2,1,0:T(8,128)(2,1)S(1)}, bf16[2,21,16,1024]{3,2,1,0:T(8,128)(2,1)S(1)}, s32[1,128]{1,0:T(1,128)S(1)}) custom-call(s32[1]{0:T(128)S(6)} %copy.14.prefix_len_hbm, s32[1]{0:T(128)S(6)} %copy.15.new_len_hbm, s32[1,5]{1,0:T(1,128)} %page_holder_hbm.1, s32[1,5]{1,0:T(1,128)} %page_slot_hbm.1, ...), custom_call_target="tpu_custom_call" | custom-call | tf_op jit(solution)/shard_map/pallas_call | solution.py:675
  45.0 1.8 %shard_map.131 = (bf16[256,4096]{1,0:T(8,128)(2,1)}, bf16[21,16,1024]{2,1,0:T(8,128)(2,1)}, bf16[21,16,1024]{2,1,0:T(8,128)(2,1)}) custom-call(bf16[256,4096]{1,0:T(8,128)(2,1)S(1)} %get-tuple-element.7.out, bf16[16,2,16,1024]{3,2,1,0:T(8,128)(2,1)S(1)} %get-tuple-element.8.recv_new, bf16[2,21,16,1024]{3,2,1,0:T(8,128)(2,1)S(1)} %get-tuple-element.9.pool, ...), custom_call_target="tpu_custom_call" | custom-call | tf_op jit(solution)/shard_map/pallas_call | solution.py:714

commit v6 on v5

--- a/solution.py
+++ b/solution.py
@@ -121,7 +121,7 @@
         pl.semaphore_signal(barrier, inc=1, device_id=(mine, peer(step)), device_id_type=MESH)
         return carry
 
-    lax.fori_loop(1, n, greet, 0)
+    lax.fori_loop(1, n, greet, 0, unroll=halves)
 
     given = [
         pltpu.make_async_copy(there, here, own_sem.at[i])
@@ -214,7 +214,11 @@
 
         lax.fori_loop(first, last, body, 0)
 
-    each(1, n, lambda step: meta_copy(step).start())
+    if halves:
+        for step in range(1, n):
+            meta_copy(step).start()
+    else:
+        each(1, n, lambda step: meta_copy(step).start())
     loads[0].wait()
     loads[1].wait()
 

time: 47 us -> 47 us (level)
  no operation moved by 1% of the time
where the time goes in v6:
time: 47 us; the launch traced here: 46.8 us
  Pallas kernels  44.9 us (96%)
  between operations  1.93 us (4%)
    pallas_call x1, Pallas kernels, shards(): pl.pallas_call(functools.partial(kernel, n, new_pages, prefix_pages), out...  43.1 us
    pallas_call x1, Pallas kernels, shards(): pl.pallas_call(finish, out_shape=results, in_specs=[held] * 4, out_specs=...  1.78 us

profile of v6, /device:TPU:1, one launch (start us, length us, event | category | flops | bytes accessed | tf_op | source)
XLA Modules:
  0.0 46.8 jit_solution(5793529837875323895)
XLA Ops:
  1.9 43.1 %shard_map.130 = (bf16[256,4096]{1,0:T(8,128)(2,1)S(1)}, bf16[16,2,16,1024]{3,2,1,0:T(8,128)(2,1)S(1)}, bf16[2,21,16,1024]{3,2,1,0:T(8,128)(2,1)S(1)}, s32[1,128]{1,0:T(1,128)S(1)}) custom-call(s32[1]{0:T(128)S(6)} %copy.14.prefix_len_hbm, s32[1]{0:T(128)S(6)} %copy.15.new_len_hbm, s32[1,5]{1,0:T(1,128)} %page_holder_hbm.1, s32[1,5]{1,0:T(1,128)} %page_slot_hbm.1, ...), custom_call_target="tpu_custom_call" | custom-call | tf_op jit(solution)/shard_map/pallas_call | solution.py:679
  45.0 1.8 %shard_map.131 = (bf16[256,4096]{1,0:T(8,128)(2,1)}, bf16[21,16,1024]{2,1,0:T(8,128)(2,1)}, bf16[21,16,1024]{2,1,0:T(8,128)(2,1)}) custom-call(bf16[256,4096]{1,0:T(8,128)(2,1)S(1)} %get-tuple-element.7.out, bf16[16,2,16,1024]{3,2,1,0:T(8,128)(2,1)S(1)} %get-tuple-element.8.recv_new, bf16[2,21,16,1024]{3,2,1,0:T(8,128)(2,1)S(1)} %get-tuple-element.9.pool, ...), custom_call_target="tpu_custom_call" | custom-call | tf_op jit(solution)/shard_map/pallas_call | solution.py:718

commit v7 on v6

--- a/solution.py
+++ b/solution.py
@@ -14,48 +14,8 @@
 ROWS = 128
 SLOT_LANE = 64
 EARLY = 5
-INNER = (
-    (("far", 0), ("far", 1)),
-    (
-        ("beside", 3),
-        ("own", 0),
-        ("mirror", 0),
-        ("layer", 1),
-        ("layer", 2),
-        ("layer", 3),
-        ("beside", 1),
-        ("far", 2),
-        ("mirror", 1),
-        ("near", 1),
-        ("near", 2),
-        ("far", 3),
-        ("beside", 2),
-        ("relay", 0),
-        ("relay", 1),
-        ("near", 3),
-    ),
-    (("beside", 0), ("near", 0)),
-)
-OUTER = (
-    (("beside", 2), ("far", 1), ("far", 2)),
-    (
-        ("own", 0),
-        ("mirror", 0),
-        ("mirror", 1),
-        ("beside", 0),
-        ("beside", 3),
-        ("beside", 1),
-        ("near", 0),
-        ("near", 3),
-        ("near", 1),
-        ("near", 2),
-        ("far", 3),
-        ("layer", 1),
-        ("layer", 2),
-        ("layer", 3),
-    ),
-    (("far", 0),),
-)
+INNER = ((('far', 0), ('far', 1)), (('beside', 3), ('own', 0), ('mirror', 0), ('layer', 1), ('layer', 2), ('layer', 3), ('beside', 1), ('far', 2), ('mirror', 1), ('near', 1), ('near', 2), ('far', 3), ('beside', 2), ('relay', 0), ('relay', 1), ('near', 3)), (('beside', 0), ('near', 0)))
+OUTER = ((('beside', 2), ('far', 1), ('far', 2)), (('own', 0), ('mirror', 0), ('mirror', 1), ('beside', 0), ('beside', 3), ('beside', 1), ('near', 0), ('near', 3), ('near', 1), ('near', 2), ('far', 3), ('layer', 1), ('layer', 2), ('layer', 3)), (('far', 0),))
 MESH = pl.DeviceIdType.MESH
 
 

time: 47 us -> 47 us (level)
  no operation moved by 1% of the time
where the time goes in v7:
time: 47 us; the launch traced here: 46.8 us
  Pallas kernels  44.9 us (96%)
  between operations  1.93 us (4%)
    pallas_call x1, Pallas kernels, shards(): pl.pallas_call(functools.partial(kernel, n, new_pages, prefix_pages), out...  43.1 us
    pallas_call x1, Pallas kernels, shards(): pl.pallas_call(finish, out_shape=results, in_specs=[held] * 4, out_specs=...  1.78 us

profile of v7, /device:TPU:1, one launch (start us, length us, event | category | flops | bytes accessed | tf_op | source)
XLA Modules:
  0.0 46.8 jit_solution(5793529837875323895)
XLA Ops:
  1.9 43.1 %shard_map.130 = (bf16[256,4096]{1,0:T(8,128)(2,1)S(1)}, bf16[16,2,16,1024]{3,2,1,0:T(8,128)(2,1)S(1)}, bf16[2,21,16,1024]{3,2,1,0:T(8,128)(2,1)S(1)}, s32[1,128]{1,0:T(1,128)S(1)}) custom-call(s32[1]{0:T(128)S(6)} %copy.14.prefix_len_hbm, s32[1]{0:T(128)S(6)} %copy.15.new_len_hbm, s32[1,5]{1,0:T(1,128)} %page_holder_hbm.1, s32[1,5]{1,0:T(1,128)} %page_slot_hbm.1, ...), custom_call_target="tpu_custom_call" | custom-call | tf_op jit(solution)/shard_map/pallas_call | solution.py:639
  45.0 1.8 %shard_map.131 = (bf16[256,4096]{1,0:T(8,128)(2,1)}, bf16[21,16,1024]{2,1,0:T(8,128)(2,1)}, bf16[21,16,1024]{2,1,0:T(8,128)(2,1)}) custom-call(bf16[256,4096]{1,0:T(8,128)(2,1)S(1)} %get-tuple-element.7.out, bf16[16,2,16,1024]{3,2,1,0:T(8,128)(2,1)S(1)} %get-tuple-element.8.recv_new, bf16[2,21,16,1024]{3,2,1,0:T(8,128)(2,1)S(1)} %get-tuple-element.9.pool, ...), custom_call_target="tpu_custom_call" | custom-call | tf_op jit(solution)/shard_map/pallas_call | solution.py:678
